TPU v7x, 32 devices: a whole 2x2x4 slice. The times are simulated.
32 devices in a mesh: row: 4 (over z), col: 8 (over y, x, core).
Axes of the slice: x: 2, y: 2, z: 4, core: 2. Of those that a mesh axis runs over, the one named last changes fastest.
Arguments:
- operator: bfloat16 [32768, 32768], P('row', 'col'), may hold values from -6 to 6
- right_test: bfloat16 [32768, 256], P('col'), may hold values from -0.03125 to 0.03125
- left_test: bfloat16 [32768, 384], P('row'), may hold values from -0.03125 to 0.03125
Outputs:
- left_factor: bfloat16 [32768, 256], P(('row', 'col'))
- right_factor: bfloat16 [32768, 256], P('col')
All inputs are finite; a program needn't handle non-finite values.
Results may differ from a plain program's by a relative error of at most 0.0015.
Values may be sent and summed in bfloat16 or wider, within the bound.
A program may use at most 192 MiB of HBM per device.

v0:
```python
import jax
import jax.numpy as jnp
from jax import lax
from jax.sharding import PartitionSpec as P


def body(operator, right_test, left_test):
    width_right = right_test.shape[1]
    block_left = jnp.dot(operator, right_test, preferred_element_type=jnp.float32)
    block_core = lax.dot_general(
        left_test.astype(jnp.float32),
        block_left,
        (((0,), (0,)), ((), ())),
        precision=lax.Precision.HIGHEST,
    )
    core_matrix = lax.psum(block_core, ("row", "col"))
    left_share = lax.psum_scatter(block_left, "col", scatter_dimension=0, tiled=True)
    right_whole = lax.psum(
        lax.dot_general(
            operator, left_test, (((0,), (0,)), ((), ())), preferred_element_type=jnp.float32
        ),
        "row",
    )
    gram_plain = jnp.dot(core_matrix.T, core_matrix, precision=lax.Precision.HIGHEST)
    shift_size = 0.001 * jnp.trace(gram_plain) / width_right
    gram_matrix = gram_plain + shift_size * jnp.eye(width_right, dtype=jnp.float32)
    lower_factor = jnp.linalg.cholesky(gram_matrix)
    solve_map = jax.scipy.linalg.cho_solve((lower_factor, True), core_matrix.T)
    right_factor = jnp.dot(right_whole, solve_map.T, precision=lax.Precision.HIGHEST).astype(
        jnp.bfloat16
    )
    return (left_share.astype(jnp.bfloat16), right_factor)


def solution(mesh):
    placed = (P("row", "col"), P("col", None), P("row", None))
    return jax.shard_map(
        body,
        mesh=mesh,
        in_specs=placed,
        out_specs=(P(("row", "col"), None), P("col", None)),
        check_vma=False,
    )
```

profile of v0, /device:TPU:0, one launch (start us, length us, event | category | flops | bytes accessed | tf_op | source)
XLA Modules:
  0.0 432.1 jit_solution(15498314063320386907)
XLA Ops:
  8.1 1.5 copy-done
  9.6 28.9 %fusion.17 = f32[8192,256]{1,0:T(8,128)} fusion(bf16[8192,4096]{1,0:T(8,128)(2,1)} %param.3, bf16[4096,256]{1,0:T(8,128)(2,1)S(1)} %copy-done), kind=kOutput, calls=%fused_computation.42 | convolution fusion | flops 17179869184 | bytes 77594624 | tf_op jit(solution)/shard_map/dot_general | solution.py:9
  38.5 10.9 %convolution_bitcast_fusion = f32[384,256]{0,1:T(8,128)} fusion(f32[8192,256]{1,0:T(8,128)} %fusion.17, bf16[8192,384]{1,0:T(8,128)(2,1)} %param.5), kind=kOutput, calls=%fused_computation.3 | convolution fusion | flops 9663676416 | bytes 15073280 | tf_op jit(solution)/shard_map/dot_general | solution.py:10
  49.4 42.3 %fusion.18 = f32[4096,384]{1,0:T(8,128)} fusion(bf16[8192,4096]{1,0:T(8,128)(2,1)} %param.3, bf16[8192,384]{1,0:T(8,128)(2,1)} %param.5), kind=kOutput, calls=%fused_computation.43 | convolution fusion | flops 25769803776 | bytes 79691776 | tf_op jit(solution)/shard_map/dot_general | solution.py:19
  91.7 0.2 reduce-scatter.2.cloned.1.call-start
  91.9 0.3 reduce-scatter.2.cloned.1.call-update
  92.3 96.1 %all-reduce.6.cloned.1.call-done = f32[384,256]{0,1:T(8,128)} async-done(((f32[384,256]{0,1:T(8,128)}), f32[384,256]{0,1:T(8,128)}) %all-reduce.6.cloned.1.call-update) | async-done | bytes 393232 | tf_op jit(solution)/shard_map/psum | solution.py:16
  188.5 2.3 select_reduce_fusion
  190.8 0.1 copy.5
  191.6 0.1 fusion.4
  191.7 11.7 %cholesky.49 = f32[128,128]{1,0:T(8,128)S(1)} custom-call(f32[128,128]{1,0:T(8,128)S(1)} %cholesky.115), custom_call_target="Cholesky" | custom-call | tf_op jit(solution)/shard_map/jit(cholesky)/cholesky | solution.py:27
  203.4 9.8 %custom-call.18 = f32[1,128,128]{1,2,0:T(8,128)S(1)} custom-call(f32[1,128,128]{2,1,0:T(8,128)S(1)} %get-tuple-element.23), custom_call_target="InvertDiagBlocksLowerTriangular" | custom-call | tf_op jit(solution)/shard_map/jit(cholesky)/cholesky | solution.py:27
  213.2 0.2 constant_dynamic-update-slice_fusion.1
  213.5 0.3 convolution_subtract_fusion.2
  213.7 11.7 %cholesky.103 = f32[128,128]{1,0:T(8,128)S(1)} custom-call(f32[128,128]{1,0:T(8,128)S(1)} %convolution_subtract_fusion.2), custom_call_target="Cholesky" | custom-call | tf_op jit(solution)/shard_map/jit(cholesky)/cholesky | solution.py:27
  225.5 0.6 compare_reduce_fusion
  227.4 0.1 triangular_solve.74
  227.4 4.0 while.1
  227.6 0.6 fusion.36
  228.2 1.3 bitcast_dynamic-update-slice_fusion.2
  229.5 0.6 fusion.36
  230.1 1.3 bitcast_dynamic-update-slice_fusion.2
  231.4 19.7 %custom-call.19 = f32[2,128,128]{1,2,0:T(8,128)S(1)} custom-call(f32[2,128,128]{2,1,0:T(8,128)S(1)} %get-tuple-element.9), custom_call_target="InvertDiagBlocksLowerTriangular" | custom-call | tf_op jit(solution)/shard_map/jit(_cho_solve)/triangular_solve | solution.py:28
  251.1 1.3 fusion.5
  252.4 1.2 convolution_subtract_fusion.1
  253.7 0.4 fusion.12
  254.0 0.3 fusion.11
  254.4 0.4 convolution_subtract_fusion
  254.7 0.3 fusion.10
  255.1 157.7 %all-reduce.4.cloned.1.call-done = f32[4096,384]{1,0:T(8,128)} async-done(((f32[4096,384]{1,0:T(8,128)}), f32[4096,384]{1,0:T(8,128)}) %all-reduce.4.cloned.1.call-update) | async-done | bytes 6291472 | tf_op jit(solution)/shard_map/psum | solution.py:18
  412.8 9.8 %convolution_convert_fusion = bf16[4096,256]{1,0:T(8,128)(2,1)} fusion(f32[4096,384]{1,0:T(8,128)} %all-reduce.4.cloned.1.call-done, f32[128,384]{1,0:T(8,128)S(1)} %fusion.11, f32[128,384]{1,0:T(8,128)S(1)} %fusion.10), kind=kOutput, calls=%fused_computation.2 | convolution fusion | flops 4832985088 | bytes 8781824 | tf_op jit(solution)/shard_map/dot_general | solution.py:29
  422.6 2.1 convert_element_type.8
  (15 shorter events, 0.3 us)
Async XLA Ops:
  8.0 1.6 copy-start
  8.0 180.4 %all-reduce.6.cloned.1.call-start = ((), (), s32[]{:S(2)}) async-start(), calls=%async_computation.3 | async-start | bytes 786432 | tf_op jit(solution)/shard_map/psum | solution.py:16
  49.3 363.5 %all-reduce.4.cloned.1.call-start = ((), (), s32[]{:S(2)}) async-start(), calls=%async_computation.2 | async-start | bytes 12582912 | tf_op jit(solution)/shard_map/psum | solution.py:18
  91.7 330.9 %reduce-scatter.2.cloned.1.call-start = ((), (), s32[]{:S(2)}) async-start(), calls=%async_computation.1 | async-start | bytes 9437184 | tf_op jit(solution)/shard_map/reduce_scatter | solution.py:17
Sparse Core Ops, SparseCore 0:
  49.5 138.9 all-reduce.5
  190.8 221.9 all-reduce.3
Sparse Core Ops, SparseCore 1:
  95.7 74.4 reduce-scatter.1
where the time goes:
time: 432 us
  waiting for transfers between devices  254 us (59%)
  matrix products  98.5 us (23%)
  other arithmetic  55.8 us (13%)
  between operations  17.5 us (4%)
  local copies, waits for them, and re-layouts  5.54 us (1%)
    psum x1, waiting for transfers between devices, body(): lax.psum(lax.dot_general(operator, left_test, (((0,), (0,)), ((), ())), p...  158 us
    psum x1, waiting for transfers between devices, body(): core_matrix = lax.psum(block_core, ('row', 'col'))  96.1 us
    dot_general x1, matrix products, body(): lax.dot_general(operator, left_test, (((0,), (0,)), ((), ())), preferred_...  42.3 us
    another operation x6, other arithmetic, body(): lower_factor = jnp.linalg.cholesky(gram_matrix)  34 us
    dot_general x1, matrix products, body(): jnp.dot(operator, right_test, preferred_element_type=jnp.float32)  28.9 us
    another operation x3, other arithmetic, body(): solve_map = jax.scipy.linalg.cho_solve((lower_factor, True), core_matrix.T)  19.7 us
    dot_general x1, matrix products, body(): lax.dot_general(left_test.astype(jnp.float32), block_left, (((0,), (0,)),...  10.9 us
    dot_general x1, matrix products, body(): jnp.dot(right_whole, solve_map.T, precision=lax.Precision.HIGHEST)  9.8 us
  transfers between devices with their start and end apart: 3, of which 2 were waited for; matrix products, arithmetic and copies ran while one was open for 27% of the time, Pallas kernels for 0%

commit v1 on v0

--- a/solution.py
+++ b/solution.py
@@ -15,11 +15,14 @@
     )
     core_matrix = lax.psum(block_core, ("row", "col"))
     left_share = lax.psum_scatter(block_left, "col", scatter_dimension=0, tiled=True)
-    right_whole = lax.psum(
-        lax.dot_general(
-            operator, left_test, (((0,), (0,)), ((), ())), preferred_element_type=jnp.float32
+    right_whole = jnp.sum(
+        lax.all_gather(
+            lax.dot_general(
+                operator, left_test, (((0,), (0,)), ((), ())), preferred_element_type=jnp.float32
+            ),
+            "row",
         ),
-        "row",
+        axis=0,
     )
     gram_plain = jnp.dot(core_matrix.T, core_matrix, precision=lax.Precision.HIGHEST)
     shift_size = 0.001 * jnp.trace(gram_plain) / width_right

time: 432 us -> 644 us (1.49)
  waiting for transfers between devices: 254 us -> 452 us
  other arithmetic: 55.8 us -> 68.6 us
    all_gather x0 -> x1, waiting for transfers between devices: none -> 357 us  [body(): lax.all_gather(lax.dot_general(operator, left_test, (((0,), (0,)), ((), (...]
    psum x1 -> x0, waiting for transfers between devices: 158 us -> none  [body(): lax.psum(lax.dot_general(operator, left_test, (((0,), (0,)), ((), ())), p...]
    reduce_sum x0 -> x1, other arithmetic: none -> 12.5 us  [body(): jnp.sum(lax.all_gather(lax.dot_general(operator, left_test, (((0,), (0,))...]
  transfers between devices with their start and end apart: 3 -> 3, of which waited for: 2 -> 2; matrix products, arithmetic and copies ran while one was open for 27% -> 17% of each run, Pallas kernels for 0% -> 0%
where the time goes in v1:
time: 644 us
  waiting for transfers between devices  452 us (70%)
  matrix products  99.2 us (15%)
  other arithmetic  68.6 us (11%)
  between operations  17.6 us (3%)
    all_gather x1, waiting for transfers between devices, body(): lax.all_gather(lax.dot_general(operator, left_test, (((0,), (0,)), ((), (...  357 us
    psum x1, waiting for transfers between devices, body(): core_matrix = lax.psum(block_core, ('row', 'col'))  95.3 us
    dot_general x1, matrix products, body(): lax.dot_general(operator, left_test, (((0,), (0,)), ((), ())), preferred_...  42.9 us
    another operation x6, other arithmetic, body(): lower_factor = jnp.linalg.cholesky(gram_matrix)  34 us
    dot_general x1, matrix products, body(): jnp.dot(operator, right_test, preferred_element_type=jnp.float32)  28.9 us
    another operation x3, other arithmetic, body(): solve_map = jax.scipy.linalg.cho_solve((lower_factor, True), core_matrix.T)  19.9 us
  transfers between devices with their start and end apart: 3, of which 2 were waited for; matrix products, arithmetic and copies ran while one was open for 17% of the time, Pallas kernels for 0%

profile of v1, /device:TPU:0, one launch (start us, length us, event | category | flops | bytes accessed | tf_op | source)
XLA Modules:
  0.0 643.8 jit_solution(4092182609931731406)
XLA Ops:
  8.1 1.5 copy-done
  9.6 28.9 %fusion.17 = f32[8192,256]{1,0:T(8,128)} fusion(bf16[8192,4096]{1,0:T(8,128)(2,1)} %param.3, bf16[4096,256]{1,0:T(8,128)(2,1)S(1)} %copy-done), kind=kOutput, calls=%fused_computation.42 | convolution fusion | flops 17179869184 | bytes 77594624 | tf_op jit(solution)/shard_map/dot_general | solution.py:9
  38.4 10.9 %convolution_bitcast_fusion = f32[384,256]{0,1:T(8,128)} fusion(f32[8192,256]{1,0:T(8,128)} %fusion.17, bf16[8192,384]{1,0:T(8,128)(2,1)} %param.5), kind=kOutput, calls=%fused_computation.3 | convolution fusion | flops 9663676416 | bytes 15073280 | tf_op jit(solution)/shard_map/dot_general | solution.py:10
  49.4 0.5 reduce-scatter.2.cloned.1.call-update
  50.0 42.9 %fusion.18 = f32[4096,384]{1,0:T(8,128)} fusion(bf16[8192,4096]{1,0:T(8,128)(2,1)} %param.3, bf16[8192,384]{1,0:T(8,128)(2,1)} %param.5), kind=kOutput, calls=%fused_computation.43 | convolution fusion | flops 25769803776 | bytes 79691776 | tf_op jit(solution)/shard_map/dot_general | solution.py:20
  92.9 95.3 %all-reduce.3.cloned.1.call-done = f32[384,256]{0,1:T(8,128)} async-done(((f32[384,256]{0,1:T(8,128)}), f32[384,256]{0,1:T(8,128)}) %all-reduce.3.cloned.1.call-update) | async-done | bytes 393232 | tf_op jit(solution)/shard_map/psum | solution.py:16
  188.2 2.3 select_reduce_fusion
  190.5 0.1 copy.5
  191.3 0.1 fusion.4
  191.4 11.7 %cholesky.49 = f32[128,128]{1,0:T(8,128)S(1)} custom-call(f32[128,128]{1,0:T(8,128)S(1)} %cholesky.115), custom_call_target="Cholesky" | custom-call | tf_op jit(solution)/shard_map/jit(cholesky)/cholesky | solution.py:30
  203.2 9.8 %custom-call.18 = f32[1,128,128]{1,2,0:T(8,128)S(1)} custom-call(f32[1,128,128]{2,1,0:T(8,128)S(1)} %get-tuple-element.23), custom_call_target="InvertDiagBlocksLowerTriangular" | custom-call | tf_op jit(solution)/shard_map/jit(cholesky)/cholesky | solution.py:30
  213.0 0.2 constant_dynamic-update-slice_fusion.1
  213.2 0.3 convolution_subtract_fusion.2
  213.5 11.7 %cholesky.103 = f32[128,128]{1,0:T(8,128)S(1)} custom-call(f32[128,128]{1,0:T(8,128)S(1)} %convolution_subtract_fusion.2), custom_call_target="Cholesky" | custom-call | tf_op jit(solution)/shard_map/jit(cholesky)/cholesky | solution.py:30
  225.2 0.7 compare_reduce_fusion
  227.3 0.1 triangular_solve.74
  227.4 4.1 while.1
  227.4 0.6 fusion.36
  228.0 1.4 bitcast_dynamic-update-slice_fusion.2
  229.5 0.6 fusion.36
  230.1 1.4 bitcast_dynamic-update-slice_fusion.2
  231.5 19.9 %custom-call.19 = f32[2,128,128]{1,2,0:T(8,128)S(1)} custom-call(f32[2,128,128]{2,1,0:T(8,128)S(1)} %get-tuple-element.9), custom_call_target="InvertDiagBlocksLowerTriangular" | custom-call | tf_op jit(solution)/shard_map/jit(_cho_solve)/triangular_solve | solution.py:31
  251.4 1.3 fusion.5
  252.7 1.2 convolution_subtract_fusion.1
  253.9 0.4 fusion.12
  254.3 0.3 fusion.11
  254.6 0.4 convolution_subtract_fusion
  255.0 0.3 fusion.10
  255.4 2.1 convert_element_type.8
  257.4 356.6 %all-gather.3.cloned.1.call-done = f32[16384,384]{1,0:T(8,128)} async-done(((f32[4096,384]{1,0:T(8,128)}), f32[16384,384]{1,0:T(8,128)}) %all-gather.3.cloned.1.call-update) | async-done | bytes 25165840 | tf_op jit(solution)/shard_map/all_gather | solution.py:19
  614.1 12.5 %reduce_sum.19 = f32[4096,384]{1,0:T(8,128)} reduce(f32[4,4096,384]{2,1,0:T(8,128)} %bitcast.51, f32[]{:T(128)} %constant.93.clone.1), dimensions={0}, to_apply=%region_1.0 | reduce | flops 4718592 | bytes 31457284 | tf_op jit(solution)/shard_map/reduce_sum | solution.py:18
  626.5 9.8 %convolution_convert_fusion = bf16[4096,256]{1,0:T(8,128)(2,1)} fusion(f32[4096,384]{1,0:T(8,128)} %reduce_sum.19, f32[128,384]{1,0:T(8,128)S(1)} %fusion.11, f32[128,384]{1,0:T(8,128)S(1)} %fusion.10), kind=kOutput, calls=%fused_computation.2 | convolution fusion | flops 4832985088 | bytes 8781824 | tf_op jit(solution)/shard_map/dot_general | solution.py:32
  (16 shorter events, 0.3 us)
Async XLA Ops:
  8.0 1.6 copy-start
  8.0 180.2 %all-reduce.3.cloned.1.call-start = ((), (), s32[]{:S(2)}) async-start(), calls=%async_computation.2 | async-start | bytes 786432 | tf_op jit(solution)/shard_map/psum | solution.py:16
  49.3 206.0 %reduce-scatter.2.cloned.1.call-start = ((), (), s32[]{:S(2)}) async-start(), calls=%async_computation.1 | async-start | bytes 9437184 | tf_op jit(solution)/shard_map/reduce_scatter | solution.py:17
  49.9 564.2 %all-gather.3.cloned.1.call-start = ((), (), s32[]{:S(2)}) async-start(), calls=%async_computation.3 | async-start | bytes 31457280 | tf_op jit(solution)/shard_map/all_gather | solution.py:19
Sparse Core Ops, SparseCore 0:
  49.4 138.7 all-reduce.2
  189.8 424.2 all-gather.2
Sparse Core Ops, SparseCore 1:
  53.3 74.4 reduce-scatter.1

commit v2 on v0

--- a/solution.py
+++ b/solution.py
@@ -13,7 +13,7 @@
         (((0,), (0,)), ((), ())),
         precision=lax.Precision.HIGHEST,
     )
-    core_matrix = lax.psum(block_core, ("row", "col"))
+    core_matrix = lax.psum(lax.psum(block_core, "row"), "col")
     left_share = lax.psum_scatter(block_left, "col", scatter_dimension=0, tiled=True)
     right_whole = lax.psum(
         lax.dot_general(

time: 432 us -> 468 us (1.083)
  waiting for transfers between devices: 254 us -> 295 us
    psum x1, waiting for transfers between devices: 158 us -> 238 us  [body(): lax.psum(lax.dot_general(operator, left_test, (((0,), (0,)), ((), ())), p...]
    psum x1, waiting for transfers between devices: 96.1 us -> 55.6 us  [body(): core_matrix = lax.psum(lax.psum(block_core, 'row'), 'col')]
  transfers between devices with their start and end apart: 3 -> 3, of which waited for: 2 -> 2; matrix products, arithmetic and copies ran while one was open for 27% -> 16% of each run, Pallas kernels for 0% -> 0%
where the time goes in v2:
time: 468 us
  waiting for transfers between devices  295 us (63%)
  matrix products  95.4 us (20%)
  other arithmetic  55.8 us (12%)
  between operations  15.8 us (3%)
  local copies, waits for them, and re-layouts  5.69 us (1%)
    psum x1, waiting for transfers between devices, body(): lax.psum(lax.dot_general(operator, left_test, (((0,), (0,)), ((), ())), p...  238 us
    psum x1, waiting for transfers between devices, body(): core_matrix = lax.psum(lax.psum(block_core, 'row'), 'col')  55.6 us
    dot_general x1, matrix products, body(): lax.dot_general(operator, left_test, (((0,), (0,)), ((), ())), preferred_...  42.4 us
    another operation x6, other arithmetic, body(): lower_factor = jnp.linalg.cholesky(gram_matrix)  34 us
    dot_general x1, matrix products, body(): jnp.dot(operator, right_test, preferred_element_type=jnp.float32)  28.9 us
    another operation x3, other arithmetic, body(): solve_map = jax.scipy.linalg.cho_solve((lower_factor, True), core_matrix.T)  19.7 us
    dot_general x1, matrix products, body(): jnp.dot(right_whole, solve_map.T, precision=lax.Precision.HIGHEST)  9.81 us
  transfers between devices with their start and end apart: 3, of which 2 were waited for; matrix products, arithmetic and copies ran while one was open for 16% of the time, Pallas kernels for 0%

profile of v2, /device:TPU:0, one launch (start us, length us, event | category | flops | bytes accessed | tf_op | source)
XLA Modules:
  0.0 467.8 jit_solution(5867249001530297164)
XLA Ops:
  7.2 1.5 copy-done
  8.8 28.9 %fusion.17 = f32[8192,256]{1,0:T(8,128)} fusion(bf16[8192,4096]{1,0:T(8,128)(2,1)} %param.3, bf16[4096,256]{1,0:T(8,128)(2,1)S(1)} %copy-done), kind=kOutput, calls=%fused_computation.42 | convolution fusion | flops 17179869184 | bytes 77594624 | tf_op jit(solution)/shard_map/dot_general | solution.py:9
  37.6 42.4 %fusion.18 = f32[4096,384]{1,0:T(8,128)} fusion(bf16[8192,4096]{1,0:T(8,128)(2,1)} %param.3, bf16[8192,384]{1,0:T(8,128)(2,1)} %param.5), kind=kOutput, calls=%fused_computation.43 | convolution fusion | flops 25769803776 | bytes 79691776 | tf_op jit(solution)/shard_map/dot_general | solution.py:19
  80.1 7.4 %convolution_bitcast_fusion = f32[384,256]{0,1:T(8,128)} fusion(f32[8192,256]{1,0:T(8,128)S(1)} %copy-done.1, bf16[8192,384]{1,0:T(8,128)(2,1)S(1)} %copy-done.2), kind=kOutput, calls=%fused_computation.3 | convolution fusion | flops 9663676416 | bytes 15073280 | tf_op jit(solution)/shard_map/dot_general | solution.py:10
  87.6 238.4 %all-reduce.7.cloned.1.call-done = (f32[4096,384]{1,0:T(8,128)}, f32[384,256]{0,1:T(8,128)}) async-done(((f32[4096,384]{1,0:T(8,128)}, f32[384,256]{0,1:T(8,128)}), (f32[4096,384]{1,0:T(8,128)}, f32[384,256]{0,1:T(8,128)})) %all-reduce.7.cloned.1.call-update) | async-done | bytes 6684688 | tf_op jit(solution)/shard_map/psum | solution.py:18
  326.1 0.3 reduce-scatter.2.cloned.1.call-start
  326.3 0.5 reduce-scatter.2.cloned.1.call-update
  326.8 55.6 %all-reduce.5.cloned.1.call-done = f32[384,256]{0,1:T(8,128)} async-done(((f32[384,256]{0,1:T(8,128)}), f32[384,256]{0,1:T(8,128)}) %all-reduce.5.cloned.1.call-update) | async-done | bytes 393232 | tf_op jit(solution)/shard_map/psum | solution.py:16
  382.4 2.5 select_reduce_fusion
  384.9 0.1 copy.5
  385.6 0.1 fusion.4
  385.7 11.7 %cholesky.49 = f32[128,128]{1,0:T(8,128)S(1)} custom-call(f32[128,128]{1,0:T(8,128)S(1)} %cholesky.115), custom_call_target="Cholesky" | custom-call | tf_op jit(solution)/shard_map/jit(cholesky)/cholesky | solution.py:27
  397.5 9.8 %custom-call.18 = f32[1,128,128]{1,2,0:T(8,128)S(1)} custom-call(f32[1,128,128]{2,1,0:T(8,128)S(1)} %get-tuple-element.25), custom_call_target="InvertDiagBlocksLowerTriangular" | custom-call | tf_op jit(solution)/shard_map/jit(cholesky)/cholesky | solution.py:27
  407.3 0.2 constant_dynamic-update-slice_fusion.1
  407.5 0.3 convolution_subtract_fusion.2
  407.8 11.7 %cholesky.103 = f32[128,128]{1,0:T(8,128)S(1)} custom-call(f32[128,128]{1,0:T(8,128)S(1)} %convolution_subtract_fusion.2), custom_call_target="Cholesky" | custom-call | tf_op jit(solution)/shard_map/jit(cholesky)/cholesky | solution.py:27
  419.5 0.7 compare_reduce_fusion
  421.5 0.1 triangular_solve.74
  421.6 4.2 while.1
  421.8 0.6 fusion.36
  422.4 1.4 bitcast_dynamic-update-slice_fusion.2
  423.8 0.6 fusion.36
  424.4 1.4 bitcast_dynamic-update-slice_fusion.2
  425.8 19.7 %custom-call.19 = f32[2,128,128]{1,2,0:T(8,128)S(1)} custom-call(f32[2,128,128]{2,1,0:T(8,128)S(1)} %get-tuple-element.9), custom_call_target="InvertDiagBlocksLowerTriangular" | custom-call | tf_op jit(solution)/shard_map/jit(_cho_solve)/triangular_solve | solution.py:28
  445.4 1.3 fusion.5
  446.7 1.2 convolution_subtract_fusion.1
  448.0 0.4 fusion.12
  448.4 0.3 fusion.11
  448.7 0.4 convolution_subtract_fusion
  449.1 0.3 fusion.10
  449.4 9.8 %convolution_convert_fusion = bf16[4096,256]{1,0:T(8,128)(2,1)} fusion(f32[4096,384]{1,0:T(8,128)} %get-tuple-element.18, f32[128,384]{1,0:T(8,128)S(1)} %fusion.11, f32[128,384]{1,0:T(8,128)S(1)} %fusion.10), kind=kOutput, calls=%fused_computation.2 | convolution fusion | flops 4832985088 | bytes 8781824 | tf_op jit(solution)/shard_map/dot_general | solution.py:29
  459.2 2.1 convert_element_type.8
  (19 shorter events, 0.3 us)
Async XLA Ops:
  7.2 1.6 copy-start
  7.2 318.9 %all-reduce.7.cloned.1.call-start = ((), (), s32[]{:S(2)}) async-start(), calls=%async_computation.3 | async-start | bytes 13369344 | tf_op jit(solution)/shard_map/psum | solution.py:18
  37.6 42.5 %copy-start.1 = (f32[8192,256]{1,0:T(8,128)S(1)}, f32[8192,256]{1,0:T(8,128)}, u32[]{:S(2)}) copy-start(f32[8192,256]{1,0:T(8,128)} %fusion.17) | copy-start | bytes 25165828
  37.6 42.5 %copy-start.2 = (bf16[8192,384]{1,0:T(8,128)(2,1)S(1)}, bf16[8192,384]{1,0:T(8,128)(2,1)}, u32[]{:S(2)}) copy-start(bf16[8192,384]{1,0:T(8,128)(2,1)} %param.5) | copy-start | bytes 18874372
  87.6 294.8 %all-reduce.5.cloned.1.call-start = ((), (), s32[]{:S(2)}) async-start(), calls=%async_computation.2 | async-start | bytes 786432 | tf_op jit(solution)/shard_map/psum | solution.py:16
  326.1 133.1 %reduce-scatter.2.cloned.1.call-start = ((), (), s32[]{:S(2)}) async-start(), calls=%async_computation.1 | async-start | bytes 9437184 | tf_op jit(solution)/shard_map/reduce_scatter | solution.py:17
Sparse Core Ops, SparseCore 0:
  87.7 238.3 all-reduce.6
  329.1 53.2 all-reduce.4
  385.9 70.9 reduce-scatter.1
